TPU v7x, 32 devices: a whole 2x2x4 slice. The times are simulated.
32 devices in a mesh: dp: 8 (over z, core), expert: 4 (over y, x).
Axes of the slice: x: 2, y: 2, z: 4, core: 2. Of those that a mesh axis runs over, the one named last changes fastest.
Arguments:
- tokens: bfloat16 [16384, 2048], P(('dp', 'expert')), parts along dimension 0, may hold values from -6 to 6
- modality: int32 [16384], P(('dp', 'expert')), parts along dimension 0, may hold values 0 or 1
- expert_ids: int32 [16384, 2], P(('dp', 'expert')), parts along dimension 0, may hold values from 0 to 3, all different within a row; in each aligned block of 512 rows (0 to 511, 512 to 1023, ...) at most 320 rows name the same one
- route_weights: float32 [16384, 2], P(('dp', 'expert')), parts along dimension 0, may hold values from 0.25 to 1
- norm_gain: float32 [2, 2048], replicated, may hold values from 0.25 to 1.75
- gate_weight: bfloat16 [2048, 3584], P(None, 'expert'), may hold values from -0.125 to 0.125
- up_weight: bfloat16 [2048, 3584], P(None, 'expert'), may hold values from -0.125 to 0.125
- down_weight: bfloat16 [3584, 2048], P('expert'), may hold values from -0.1875 to 0.1875
Outputs:
- mixed: bfloat16 [16384, 2048], P(('dp', 'expert')), parts along dimension 0
There are 8 independent parts, one for each index of `dp`. A program takes and returns all parts, laid end to end along the dimension named above; an argument that names none is the same for every part. Nothing has to cross between parts.
Inputs may be any that keep to these rules, and one draw needn't show every extreme that they name: `expert_ids`: each row names 2 different experts. Among the rows of one device no expert is named by more than 320 rows, a bound that some blocks reach.
All inputs are finite; a program needn't handle non-finite values. No bound on the sum of `modality` on one device may be relied on, other than what follows from the above.
Results may differ from a plain program's by a relative error of at most 0.0054.
Values may be sent and summed in bfloat16 or wider, within the bound.
A program may use at most 128 MiB of HBM per device.

v0:
```python
import jax
import jax.numpy as jnp
from jax import lax
from jax.sharding import PartitionSpec as P

epsilon = 1e-05


def normalize(tokens, modality, norm_gain):
    values = tokens.astype(jnp.float32)
    square = jnp.mean(values * values, axis=1, keepdims=True)
    gains = jnp.where(modality[:, None] == 1, norm_gain[1][None, :], norm_gain[0][None, :])
    return (values * lax.rsqrt(square + epsilon) * gains).astype(jnp.bfloat16)


def slot_table(expert_ids, experts, capacity):
    fanout = expert_ids.shape[1]
    flat_ids = expert_ids.reshape(-1)
    columns = jnp.arange(experts, dtype=jnp.int32)
    onehot = (flat_ids[:, None] == columns[None, :]).astype(jnp.int32)
    earlier = jnp.cumsum(onehot, axis=0) - onehot
    position = jnp.sum(earlier * onehot, axis=1)
    slots = flat_ids * capacity + position
    sources = jnp.arange(flat_ids.shape[0], dtype=jnp.int32) // fanout
    owners = jnp.full((experts * capacity,), -1, jnp.int32).at[slots].set(sources)
    return (slots, owners)


def pack_rows(normed, owners):
    chosen = jnp.take(normed, jnp.maximum(owners, 0), axis=0)
    return jnp.where(owners[:, None] >= 0, chosen, jnp.zeros_like(chosen))


def expert_rows(rows, gate_weight, up_weight, down_weight):
    leading = rows.shape[:-1]
    flat = rows.reshape(-1, rows.shape[-1])
    gate = jnp.dot(flat, gate_weight, preferred_element_type=jnp.float32)
    upper = jnp.dot(flat, up_weight, preferred_element_type=jnp.float32)
    active = (jax.nn.silu(gate) * upper).astype(jnp.bfloat16)
    result = jnp.dot(active, down_weight, preferred_element_type=jnp.float32).astype(jnp.bfloat16)
    return result.reshape(leading + (down_weight.shape[1],))


def shards(
    tokens, modality, expert_ids, route_weights, norm_gain, gate_weight, up_weight, down_weight
):
    devices = lax.axis_size("expert")
    tok_rows, width = tokens.shape
    fanout = expert_ids.shape[1]
    capacity = min(tok_rows, tok_rows * fanout * 5 // (4 * devices))
    normed = normalize(tokens, modality, norm_gain)
    slots, owners = slot_table(expert_ids, devices, capacity)
    blocks = pack_rows(normed, owners).reshape(devices, capacity, width)
    finished = expert_rows(
        lax.all_to_all(blocks, "expert", split_axis=0, concat_axis=0, tiled=True),
        gate_weight,
        up_weight,
        down_weight,
    )
    returned = lax.all_to_all(finished, "expert", split_axis=0, concat_axis=0, tiled=True)
    expert_out = returned.reshape(devices * capacity, width)
    picked = (
        jnp.take(expert_out, slots, axis=0).reshape(tok_rows, fanout, width).astype(jnp.float32)
    )
    mixed = tokens.astype(jnp.float32) + jnp.sum(route_weights[:, :, None] * picked, axis=1)
    return mixed.astype(jnp.bfloat16)


def solution(mesh):
    placed = (
        P(("dp", "expert"), None),
        P(("dp", "expert")),
        P(("dp", "expert"), None),
        P(("dp", "expert"), None),
        P(),
        P(None, "expert"),
        P(None, "expert"),
        P("expert", None),
    )
    return jax.shard_map(
        shards, mesh=mesh, in_specs=placed, out_specs=P(("dp", "expert"), None), check_vma=False
    )
```

profile of v0, /device:TPU:0, one launch (start us, length us, event | category | flops | bytes accessed | tf_op | source)
XLA Modules:
  0.0 219.0 jit_solution(7238481432283802018)
XLA Ops:
  0.0 0.8 copy.16
  0.8 0.2 eq.33
  1.0 0.2 reshape.101
  1.2 0.7 broadcast_multiply_fusion
  1.9 1.1 reduce-window.6
  3.0 0.2 slice_reduce_fusion
  3.2 0.2 reduce-window.9
  3.5 0.2 copy.20
  3.7 0.2 mul.55
  3.9 4.3 %scatter_custom_fusion = s32[1280]{0:T(1024)S(1)} fusion(s32[1024]{0:T(1024)S(1)} %bitcast.39, s32[1024]{0:T(1024)S(1)} %add_select_fusion, s32[]{:T(128)} %constant.62.clone.1), kind=kCustom, calls=%fused_computation.37 | custom fusion | bytes 5124 | tf_op jit(solution)/shard_map/scatter | solution.py:25
  8.3 0.8 fusion.14
  9.1 2.1 fusion
  11.2 0.7 broadcast_compare_fusion.2
  11.8 0.1 broadcast_in_dim.76
  11.9 0.1 broadcast_in_dim.78
  12.0 2.4 %fusion.2 = bf16[512,2048]{1,0:T(8,128)(2,1)S(1)} fusion(bf16[512,2048]{1,0:T(8,128)(2,1)} %param.8, f32[2048]{0:T(1024)S(1)} %bitcast.38, f32[2048]{0:T(1024)S(1)} %bitcast.37, f32[512]{0:T(512)S(1)} %add_rsqrt_fusion, pred[512]{0:T(512)(128)(4,1)S(1)} %broadcast_compare_fusion.2), kind=kLoop, calls=%fused_computation.13 | loop fusion | flops 5242880 | bytes 4213248 | tf_op jit(solution)/shard_map/convert_element_type | solution.py:13
  14.4 6.1 %gather_fusion = bf16[1280,2048]{1,0:T(8,128)(2,1)} fusion(bf16[512,2048]{1,0:T(8,128)(2,1)S(1)} %fusion.2, s32[2048]{0:T(1024)S(1)} %pad_clamp_fusion), kind=kCustom, calls=%fused_computation | custom fusion | bytes 10490880 | tf_op jit(solution)/shard_map/jit(_take)/gather | solution.py:30
  20.5 3.7 %select_select_fusion = bf16[4,320,2048]{2,1,0:T(8,128)(2,1)S(1)} fusion(bf16[4,320,2048]{2,1,0:T(8,128)(2,1)} %bitcast.32, pred[4,320]{1,0:T(4,128)(4,1)S(1)} %broadcast_in_dim.78, pred[4,320]{1,0:T(4,128)(4,1)S(1)} %broadcast_in_dim.76), kind=kLoop, calls=%fused_computation.9 | loop fusion | flops 5242880 | bytes 10488320 | tf_op jit(solution)/shard_map/jit(_where)/select_n | solution.py:31
  24.3 64.3 %all_to_all.10 = bf16[4,320,2048]{2,1,0:T(8,128)(2,1)S(1)} all-to-all(bf16[4,320,2048]{2,1,0:T(8,128)(2,1)S(1)} %select_select_fusion), channel_id=1, replica_groups=mesh['dp'=8,'expert'=4] {'expert'}, dimensions={0} | all-to-all | bytes 10485760 | tf_op jit(solution)/shard_map/all_to_all | solution.py:55
  88.6 2.3 %copy-done.1 = bf16[4,320,2048]{2,1,0:T(8,128)(2,1)} copy-done((bf16[4,320,2048]{2,1,0:T(8,128)(2,1)}, bf16[4,320,2048]{2,1,0:T(8,128)(2,1)S(1)}, u32[]{:S(2)}) %copy-start.1) | copy-done | bytes 5242904
  91.0 7.1 %fusion.15 = f32[1280,896]{1,0:T(8,128)} fusion(bf16[1280,2048]{1,0:T(8,128)(2,1)S(1)} %bitcast.34, bf16[2048,896]{1,0:T(8,128)(2,1)S(1)} %copy-done.4), kind=kOutput, calls=%fused_computation.46 | convolution fusion | flops 4697620480 | bytes 13500416 | tf_op jit(solution)/shard_map/dot_general | solution.py:37
  98.1 17.5 %convolution_convert_fusion = bf16[1280,2048]{1,0:T(8,128)(2,1)} fusion(bf16[896,2048]{1,0:T(8,128)(2,1)} %param.15, f32[1280,896]{1,0:T(8,128)} %fusion.15, bf16[1280,2048]{1,0:T(8,128)(2,1)} %bitcast.35, bf16[2048,896]{1,0:T(8,128)(2,1)} %param.14), kind=kOutput, calls=%fused_computation.5 | convolution fusion | flops 9404743680 | bytes 22413312 | tf_op jit(solution)/shard_map/dot_general | solution.py:40
  115.6 5.4 %all-to-all-start.1 = ((bf16[4,320,2048]{2,1,0:T(8,128)(2,1)}), bf16[4,320,2048]{2,1,0:T(8,128)(2,1)}, u32[]{:S(2)}, u32[]{:S(2)}) async-start(bf16[4,320,2048]{2,1,0:T(8,128)(2,1)} %bitcast.33), calls=%async_computation.1 | async-start | bytes 10485760 | tf_op jit(solution)/shard_map/all_to_all | solution.py:60
  121.0 0.2 reduce_sum.32
  121.2 0.1 copy.18
  121.4 0.2 copy.19
  121.6 0.1 copy.15
  121.7 56.5 %all-to-all-done.1 = bf16[4,320,2048]{2,1,0:T(8,128)(2,1)} async-done(((bf16[4,320,2048]{2,1,0:T(8,128)(2,1)}), bf16[4,320,2048]{2,1,0:T(8,128)(2,1)}, u32[]{:S(2)}, u32[]{:S(2)}) %all-to-all-start.1) | async-done | bytes 5242912 | tf_op jit(solution)/shard_map/all_to_all | solution.py:60
  178.3 12.0 %gather_fusion.1 = bf16[1024,2048]{1,0:T(8,128)(2,1)} fusion(bf16[1280,2048]{1,0:T(8,128)(2,1)} %bitcast.8, s32[1024]{0:T(1024)S(1)} %broadcast_clamp_fusion), kind=kCustom, calls=%fused_computation.1 | custom fusion | bytes 8392704 | tf_op jit(solution)/shard_map/jit(_take)/gather | solution.py:63
  190.3 7.6 %gather.15 = bf16[512,2,2048]{2,1,0:T(2,128)(2,1)} reshape(bf16[1024,2048]{1,0:T(8,128)(2,1)} %gather_fusion.1) | data formatting | bytes 8388608 | tf_op jit(solution)/shard_map/jit(_take)/gather | solution.py:63
  197.9 19.0 %multiply_reduce_fusion = f32[512,2048]{1,0:T(8,128)S(1)} fusion(bf16[512,2,2048]{2,1,0:T(2,128)(2,1)} %gather.15, pred[512,2]{1,0:T(8,128)(4,1)S(1)} %copy.19, f32[512,2]{1,0:T(8,128)S(1)} %copy.15), kind=kLoop, calls=%fused_computation.3 | loop fusion | flops 7340032 | bytes 8393728 | tf_op jit(solution)/shard_map/reduce_sum | solution.py:65
  216.9 2.1 fusion.3
  (20 shorter events, 0.2 us)
Async XLA Ops:
  24.3 66.7 %copy-start.4 = (bf16[2048,896]{1,0:T(8,128)(2,1)S(1)}, bf16[2048,896]{1,0:T(8,128)(2,1)}, u32[]{:S(2)}) copy-start(bf16[2048,896]{1,0:T(8,128)(2,1)} %param.13) | copy-start | bytes 11010052
  88.6 2.3 %copy-start.1 = (bf16[4,320,2048]{2,1,0:T(8,128)(2,1)}, bf16[4,320,2048]{2,1,0:T(8,128)(2,1)S(1)}, u32[]{:S(2)}) copy-start(bf16[4,320,2048]{2,1,0:T(8,128)(2,1)S(1)} %all_to_all.10) | copy-start | bytes 15728644
  115.6 5.7 %copy-start.2 = (s32[512,2]{0,1:T(2,128)S(1)}, s32[512,2]{0,1:T(2,128)}, u32[]{:S(2)}) copy-start(s32[512,2]{0,1:T(2,128)} %param.10) | copy-start | bytes 12292
  115.6 5.9 %copy-start.3 = (f32[512,2]{0,1:T(2,128)S(1)}, f32[512,2]{0,1:T(2,128)}, u32[]{:S(2)}) copy-start(f32[512,2]{0,1:T(2,128)} %param.11) | copy-start | bytes 12292
  115.6 62.7 %all-to-all-start.1 = ((bf16[4,320,2048]{2,1,0:T(8,128)(2,1)}), bf16[4,320,2048]{2,1,0:T(8,128)(2,1)}, u32[]{:S(2)}, u32[]{:S(2)}) async-start(bf16[4,320,2048]{2,1,0:T(8,128)(2,1)} %bitcast.33), calls=%async_computation.1 | async-start | bytes 10485760 | tf_op jit(solution)/shard_map/all_to_all | solution.py:60
  197.9 19.0 %copy-start = (bf16[512,2048]{1,0:T(8,128)(2,1)S(1)}, bf16[512,2048]{1,0:T(8,128)(2,1)}, u32[]{:S(2)}) copy-start(bf16[512,2048]{1,0:T(8,128)(2,1)} %param.8) | copy-start | bytes 6291460
where the time goes:
time: 220 us; the launch traced here: 219 us
  blocking collectives  64.3 us (29%)
  waiting for transfers between devices  56.5 us (26%)
  local copies, waits for them, and re-layouts  35.8 us (16%)
  other arithmetic  32.1 us (15%)
  matrix products  24.7 us (11%)
  starting transfers between devices  5.39 us (2%)
    all_to_all x1, blocking collectives, shards(): lax.all_to_all(blocks, 'expert', split_axis=0, concat_axis=0, tiled=True)  64.3 us
    all_to_all x1, waiting for transfers between devices, shards(): lax.all_to_all(finished, 'expert', split_axis=0, concat_axis=0, tiled=True)  56.5 us
    gather x2, local copies, waits for them, and re-layouts, shards(): jnp.take(expert_out, slots, axis=0).reshape(tok_rows, fanout, width)  19.6 us
    reduce_sum x1, other arithmetic, shards(): jnp.sum(route_weights[:, :, None] * picked, axis=1)  19 us
    dot_general x1, matrix products, expert_rows(): jnp.dot(active, down_weight, preferred_element_type=jnp.float32)  17.5 us
    dot_general x1, matrix products, expert_rows(): gate = jnp.dot(flat, gate_weight, preferred_element_type=jnp.float32)  7.15 us
    gather x1, local copies, waits for them, and re-layouts, pack_rows(): chosen = jnp.take(normed, jnp.maximum(owners, 0), axis=0)  6.12 us
    all_to_all x1, starting transfers between devices, shards(): lax.all_to_all(finished, 'expert', split_axis=0, concat_axis=0, tiled=True)  5.39 us
  transfers between devices with their start and end apart: 1, of which 1 were waited for; matrix products, arithmetic and copies ran while one was open for 0% of the time, Pallas kernels for 0%

commit v1 on v0

v1 whole, which is shorter than its diff:
```python
import functools

import jax
import jax.numpy as jnp
from jax import lax
from jax.experimental import pallas as pl
from jax.experimental.pallas import tpu as pltpu
from jax.sharding import PartitionSpec as P

epsilon = 1e-05
LANES = 128
AXIS = "expert"


def grid_side(devices):
    side = 1
    while side * side < devices:
        side += 1
    return side if side * side == devices else devices


def moe_kernel(
    devices,
    tokens_hbm,
    modality_ref,
    ids_ref,
    weights_ref,
    gain_ref,
    gate_hbm,
    up_hbm,
    down_hbm,
    out_ref,
    tokens,
    gate,
    up,
    down,
    normed,
    total,
    place_rows,
    place_cols,
    share_cols,
    packed,
    arrived,
    finished,
    returned,
    load_sem,
    go_send,
    go_recv,
    back_send,
    back_recv,
):
    waves, _, chunk, width = packed.shape
    tok_rows = tokens.shape[0]
    fanout = ids_ref.shape[0]
    me = lax.axis_index(AXIS)
    side = grid_side(devices)
    mine_hi, mine_lo = me // side, me % side
    lines = devices // side

    def ahead(step):
        return ((mine_hi + step // side) % lines) * side + (mine_lo + step % side) % side

    def behind(step):
        return ((mine_hi + lines - step // side) % lines) * side + (
            mine_lo + side - step % side
        ) % side

    def go(wave, step):
        return pltpu.make_async_remote_copy(
            src_ref=packed.at[wave, step],
            dst_ref=arrived.at[wave, step],
            send_sem=go_send.at[wave, step],
            recv_sem=go_recv.at[wave, step],
            device_id={AXIS: ahead(step)},
            device_id_type=pl.DeviceIdType.MESH,
        )

    def back(wave, step):
        return pltpu.make_async_remote_copy(
            src_ref=finished.at[wave, step],
            dst_ref=returned.at[wave, step],
            send_sem=back_send.at[wave, step],
            recv_sem=back_recv.at[wave, step],
            device_id={AXIS: behind(step)},
            device_id_type=pl.DeviceIdType.MESH,
        )

    loads = [
        pltpu.make_async_copy(tokens_hbm, tokens, load_sem.at[0]),
        pltpu.make_async_copy(gate_hbm, gate, load_sem.at[1]),
        pltpu.make_async_copy(up_hbm, up, load_sem.at[2]),
        pltpu.make_async_copy(down_hbm, down, load_sem.at[3]),
    ]
    for load in loads:
        load.start()

    barrier = pltpu.get_barrier_semaphore()

    def greet(step, carry):
        pl.semaphore_signal(
            barrier, inc=1, device_id={AXIS: ahead(step)}, device_id_type=pl.DeviceIdType.MESH
        )
        return carry

    lax.fori_loop(1, devices, greet, 0)

    expert = lax.broadcasted_iota(jnp.int32, (LANES, tok_rows), 0)
    named = jnp.zeros((LANES, tok_rows), jnp.float32)
    share = jnp.zeros((LANES, tok_rows), jnp.float32)
    for k in range(fanout):
        hit = expert == ids_ref[k : k + 1, :]
        named = jnp.where(hit, 1.0, named)
        share = jnp.where(hit, weights_ref[k : k + 1, :], share)
    before = (
        lax.broadcasted_iota(jnp.int32, (tok_rows, tok_rows), 0)
        < lax.broadcasted_iota(jnp.int32, (tok_rows, tok_rows), 1)
    )
    count = jnp.dot(
        named.astype(jnp.bfloat16),
        jnp.where(before, 1.0, 0.0).astype(jnp.bfloat16),
        preferred_element_type=jnp.float32,
    )
    place = jnp.where(named > 0.5, count, -1.0)
    place_rows[...] = place
    place_cols[...] = place.T
    share_cols[...] = share.T
    image = jnp.broadcast_to(modality_ref[...].astype(jnp.float32), (LANES, tok_rows)).T

    loads[0].wait()
    rows = 64
    for start in range(0, tok_rows, rows):
        values = tokens[start : start + rows, :].astype(jnp.float32)
        square = jnp.mean(values * values, axis=1, keepdims=True)
        gains = jnp.where(
            image[start : start + rows, :1] > 0.5, gain_ref[1:2, :], gain_ref[0:1, :]
        )
        normed[start : start + rows, :] = (
            values * lax.rsqrt(square + epsilon) * gains
        ).astype(jnp.bfloat16)

    def pack(wave, step, target):
        line = place_rows[pl.ds(ahead(step), 1), :]
        slot = lax.broadcasted_iota(jnp.int32, (chunk, tok_rows), 0) + wave * chunk
        pick = jnp.where(line == slot.astype(jnp.float32), 1.0, 0.0).astype(jnp.bfloat16)
        target[wave, step] = jnp.dot(
            pick, normed[...], preferred_element_type=jnp.float32
        ).astype(jnp.bfloat16)

    others = devices - 1
    items = waves * others

    def which(item):
        return item // others, others - item % others

    pl.semaphore_wait(barrier, others)

    def send(item, carry):
        wave, step = which(item)
        pack(wave, step, packed)
        go(wave, step).start()
        return carry

    lax.fori_loop(0, items, send, 0)

    for load in loads[1:]:
        load.wait()

    def feed(source, target, wave, step):
        value = source[wave, step]
        opened = jnp.dot(value, gate[...], preferred_element_type=jnp.float32)
        upper = jnp.dot(value, up[...], preferred_element_type=jnp.float32)
        active = (opened / (1.0 + jnp.exp(-opened)) * upper).astype(jnp.bfloat16)
        target[wave, step] = jnp.dot(
            active, down[...], preferred_element_type=jnp.float32
        ).astype(jnp.bfloat16)

    def spread(wave, step):
        lane = lax.broadcasted_iota(jnp.int32, (tok_rows, LANES), 1) == ahead(step)
        line = jnp.sum(jnp.where(lane, place_cols[...], 0.0), axis=1, keepdims=True)
        worth = jnp.sum(jnp.where(lane, share_cols[...], 0.0), axis=1, keepdims=True)
        slot = lax.broadcasted_iota(jnp.int32, (tok_rows, chunk), 1) + wave * chunk
        spots = jnp.where(line == slot.astype(jnp.float32), worth, 0.0)
        high = spots.astype(jnp.bfloat16)
        low = (spots - high.astype(jnp.float32)).astype(jnp.bfloat16)
        value = returned[wave, step]
        return jnp.dot(high, value, preferred_element_type=jnp.float32) + jnp.dot(
            low, value, preferred_element_type=jnp.float32
        )

    total[...] = tokens[...].astype(jnp.float32)

    def local(wave, carry):
        pack(wave, 0, arrived)
        feed(arrived, returned, wave, 0)
        total[...] += spread(wave, 0)
        return carry

    lax.fori_loop(0, waves, local, 0)

    def serve(item, carry):
        wave, step = which(item)
        go(wave, step).wait_recv()
        feed(arrived, finished, wave, step)
        back(wave, step).start()
        return carry

    lax.fori_loop(0, items, serve, 0)

    def collect(item, carry):
        wave, step = which(item)
        back(wave, step).wait_recv()
        total[...] += spread(wave, step)
        return carry

    lax.fori_loop(0, items - 1, collect, 0)
    wave, step = which(items - 1)
    back(wave, step).wait_recv()
    out_ref[...] = (total[...] + spread(wave, step)).astype(out_ref.dtype)

    def settle(item, carry):
        wave, step = which(item)
        go(wave, step).wait_send()
        back(wave, step).wait_send()
        return carry

    lax.fori_loop(0, items, settle, 0)


def shards(
    tokens, modality, expert_ids, route_weights, norm_gain, gate_weight, up_weight, down_weight
):
    devices = lax.axis_size(AXIS)
    tok_rows, width = tokens.shape
    fanout = expert_ids.shape[1]
    hidden = gate_weight.shape[1]
    capacity = min(tok_rows, tok_rows * fanout * 5 // (4 * devices))
    waves = 2 if capacity % 32 == 0 and capacity >= 256 else 1
    chunk = capacity // waves
    buffer = pltpu.VMEM((waves, devices, chunk, width), jnp.bfloat16)
    near = pl.BlockSpec(memory_space=pltpu.VMEM)
    far = pl.BlockSpec(memory_space=pl.ANY)
    sems = pltpu.SemaphoreType.DMA((waves, devices))
    return pl.pallas_call(
        functools.partial(moe_kernel, devices),
        out_shape=jax.ShapeDtypeStruct((tok_rows, width), jnp.bfloat16),
        in_specs=[far, near, near, near, near, far, far, far],
        out_specs=near,
        scratch_shapes=[
            pltpu.VMEM((tok_rows, width), jnp.bfloat16),
            pltpu.VMEM((width, hidden), jnp.bfloat16),
            pltpu.VMEM((width, hidden), jnp.bfloat16),
            pltpu.VMEM((hidden, width), jnp.bfloat16),
            pltpu.VMEM((tok_rows, width), jnp.bfloat16),
            pltpu.VMEM((tok_rows, width), jnp.float32),
            pltpu.VMEM((LANES, tok_rows), jnp.float32),
            pltpu.VMEM((tok_rows, LANES), jnp.float32),
            pltpu.VMEM((tok_rows, LANES), jnp.float32),
            buffer,
            buffer,
            buffer,
            buffer,
            pltpu.SemaphoreType.DMA((4,)),
            sems,
            sems,
            sems,
            sems,
        ],
        compiler_params=pltpu.CompilerParams(
            collective_id=0, has_side_effects=True, vmem_limit_bytes=62 * 1024 * 1024
        ),
    )(
        tokens,
        modality.reshape(1, tok_rows),
        expert_ids.T,
        route_weights.T,
        norm_gain,
        gate_weight,
        up_weight,
        down_weight,
    )


def solution(mesh):
    placed = (
        P(("dp", AXIS), None),
        P(("dp", AXIS)),
        P(("dp", AXIS), None),
        P(("dp", AXIS), None),
        P(),
        P(None, AXIS),
        P(None, AXIS),
        P(AXIS, None),
    )
    return jax.shard_map(
        shards, mesh=mesh, in_specs=placed, out_specs=P(("dp", AXIS), None), check_vma=False
    )
```

time: 220 us -> 128 us (0.58)
  Pallas kernels: 0 us -> 125 us
  blocking collectives: 64.3 us -> 0 us
  waiting for transfers between devices: 56.5 us -> 0 us
  local copies, waits for them, and re-layouts: 35.8 us -> 3.16 us
  other arithmetic: 32.1 us -> 0 us
  matrix products: 24.7 us -> 0 us
  starting transfers between devices: 5.39 us -> 0 us
    pallas_call x0 -> x1, Pallas kernels: none -> 125 us  [shards(): pl.pallas_call(functools.partial(moe_kernel, devices), out_shape=jax.Shap...]
    all_to_all x1 -> x0, blocking collectives: 64.3 us -> none  [shards(): lax.all_to_all(blocks, 'expert', split_axis=0, concat_axis=0, tiled=True)]
    all_to_all x1 -> x0, waiting for transfers between devices: 56.5 us -> none  [shards(): lax.all_to_all(finished, 'expert', split_axis=0, concat_axis=0, tiled=True)]
    gather x3 -> x0, local copies, waits for them, and re-layouts: 25.7 us -> none  [the longest x2 19.6 us: shards(): jnp.take(expert_out, slots, axis=0).reshape(tok_rows, fanout, width)]
    dot_general x2 -> x0, matrix products: 24.7 us -> none  [the longest x1 17.5 us: expert_rows(): jnp.dot(active, down_weight, preferred_element_type=jnp.float32)]
    reduce_sum x3 -> x0, other arithmetic: 21.1 us -> none  [the longest x1 19 us: shards(): jnp.sum(route_weights[:, :, None] * picked, axis=1)]
    all_to_all x1 -> x0, starting transfers between devices: 5.39 us -> none  [shards(): lax.all_to_all(finished, 'expert', split_axis=0, concat_axis=0, tiled=True)]
    convert_element_type x3 -> x0, other arithmetic: 4.47 us -> none  [the longest x1 2.4 us: normalize(): return (values * lax.rsqrt(square + epsilon) * gains).astype(jnp.bfloat16)]
  transfers between devices with their start and end apart: 1 -> 0, of which waited for: 1 -> 0; matrix products, arithmetic and copies ran while one was open for 0% -> 0% of each run, Pallas kernels for 0% -> 0%
where the time goes in v1:
time: 128 us
  Pallas kernels  125 us (98%)
  local copies, waits for them, and re-layouts  3.16 us (2%)
    pallas_call x1, Pallas kernels, shards(): pl.pallas_call(functools.partial(moe_kernel, devices), out_shape=jax.Shap...  125 us
    unnamed x1, local copies, waits for them, and re-layouts  3.16 us

profile of v1, /device:TPU:0, one launch (start us, length us, event | category | flops | bytes accessed | tf_op | source)
XLA Modules:
  0.0 128.1 jit_solution(2437379887365949526)
XLA Ops:
  0.0 124.9 %shard_map.82 = bf16[512,2048]{1,0:T(8,128)(2,1)} custom-call(bf16[512,2048]{1,0:T(8,128)(2,1)} %tokens_hbm.1, s32[1,512]{1,0:T(1,128)} %bitcast.5, s32[2,512]{1,0:T(2,128)} %bitcast.3, f32[2,512]{1,0:T(2,128)} %bitcast.4, f32[2,2048]{1,0:T(2,128)} %gain_ref.1, bf16[2048,896]{1,0:T(8,128)(2,1)} %gate_hbm.1, bf16[2048,896]{1,0:T(8,128)(2,1)} %up_hbm.1, ...), custom_call_target="tpu_custom_call" | custom-call | tf_op jit(solution)/shard_map/pallas_call | solution.py:243
  124.9 3.2 %copy.10 = bf16[512,2048]{1,0:T(8,128)(2,1)} copy(bf16[512,2048]{1,0:T(8,128)(2,1)} %shard_map.82) | data formatting | bytes 4194304

commit v2 on v1

--- a/solution.py
+++ b/solution.py
@@ -226,6 +226,318 @@
     lax.fori_loop(0, items, settle, 0)
 
 
+def relay_kernel(
+    blocks,
+    tokens_hbm,
+    modality_ref,
+    ids_ref,
+    weights_ref,
+    gain_ref,
+    gate_hbm,
+    up_hbm,
+    down_hbm,
+    out_ref,
+    tokens,
+    near_tokens,
+    gate,
+    up,
+    down,
+    normed,
+    near_normed,
+    total,
+    near_total,
+    facts,
+    near_facts,
+    packed,
+    arrived,
+    finished,
+    returned,
+    own_rows,
+    own_results,
+    sum_out,
+    sum_in,
+    load_sem,
+    facts_sem,
+    dense_send,
+    dense_recv,
+    go_send,
+    go_recv,
+    back_send,
+    back_recv,
+    sum_send,
+    sum_recv,
+):
+    _, capacity, width = packed.shape
+    waves = go_send.shape[1]
+    chunk = capacity // waves
+    tok_rows = tokens.shape[0]
+    part = tok_rows // blocks
+    fanout = ids_ref.shape[0]
+    me = lax.axis_index(AXIS)
+    role = lax.axis_index("dp") % 2
+    high, low = me // 2, me % 2
+    beside = high * 2 + 1 - low
+    above = (1 - high) * 2 + low
+    first = beside * (1 - role) + above * role
+    second = above * (1 - role) + beside * role
+
+    def remote(source, target, send_sem, recv_sem, peer):
+        return pltpu.make_async_remote_copy(
+            src_ref=source,
+            dst_ref=target,
+            send_sem=send_sem,
+            recv_sem=recv_sem,
+            device_id={AXIS: peer},
+            device_id_type=pl.DeviceIdType.MESH,
+        )
+
+    def part_rows(block):
+        return pl.ds(pl.multiple_of(block * part, part), part)
+
+    def wave_rows(wave):
+        return pl.ds(pl.multiple_of(wave * chunk, chunk), chunk)
+
+    def dense(block):
+        rows = part_rows(block)
+        return remote(
+            tokens.at[rows], near_tokens.at[rows], dense_send.at[block], dense_recv.at[block], first
+        )
+
+    def go(kind, wave):
+        rows = wave_rows(wave)
+        return remote(
+            packed.at[kind, rows],
+            arrived.at[kind, rows],
+            go_send.at[kind, wave],
+            go_recv.at[kind, wave],
+            second,
+        )
+
+    def back(kind, wave):
+        rows = wave_rows(wave)
+        return remote(
+            finished.at[kind, rows],
+            returned.at[kind, rows],
+            back_send.at[kind, wave],
+            back_recv.at[kind, wave],
+            second,
+        )
+
+    def sums(block):
+        rows = part_rows(block)
+        return remote(
+            sum_out.at[rows], sum_in.at[rows], sum_send.at[block], sum_recv.at[block], first
+        )
+
+    def each(count, step):
+        def body(index, carry):
+            step(index)
+            return carry
+
+        lax.fori_loop(0, count, body, 0)
+
+    loads = [
+        pltpu.make_async_copy(tokens_hbm, tokens, load_sem.at[0]),
+        pltpu.make_async_copy(gate_hbm, gate, load_sem.at[1]),
+        pltpu.make_async_copy(up_hbm, up, load_sem.at[2]),
+        pltpu.make_async_copy(down_hbm, down, load_sem.at[3]),
+    ]
+    loads[0].start()
+    barrier = pltpu.get_barrier_semaphore()
+    for peer in (first, second):
+        pl.semaphore_signal(
+            barrier, inc=1, device_id={AXIS: peer}, device_id_type=pl.DeviceIdType.MESH
+        )
+    loads[0].wait()
+    pl.semaphore_wait(barrier, 2)
+    each(blocks, lambda block: dense(block).start())
+    for load in loads[1:]:
+        load.start()
+
+    lines = 8
+    expert = lax.broadcasted_iota(jnp.int32, (lines, tok_rows), 0)
+    named = jnp.zeros((lines, tok_rows), jnp.float32)
+    share = jnp.zeros((lines, tok_rows), jnp.float32)
+    for k in range(fanout):
+        hit = expert == ids_ref[k : k + 1, :]
+        named = jnp.where(hit, 1.0, named)
+        share = jnp.where(hit, weights_ref[k : k + 1, :], share)
+    before = (
+        lax.broadcasted_iota(jnp.int32, (tok_rows, tok_rows), 0)
+        < lax.broadcasted_iota(jnp.int32, (tok_rows, tok_rows), 1)
+    )
+    count = jnp.dot(
+        named.astype(jnp.bfloat16),
+        jnp.where(before, 1.0, 0.0).astype(jnp.bfloat16),
+        preferred_element_type=jnp.float32,
+    )
+    facts[0:lines, :] = jnp.where(named > 0.5, count, -1.0)
+    facts[lines : 2 * lines, :] = share
+    facts[2 * lines : 3 * lines, :] = jnp.broadcast_to(
+        modality_ref[...].astype(jnp.float32), (lines, tok_rows)
+    )
+    told = remote(facts, near_facts, facts_sem.at[0], facts_sem.at[1], first)
+    told.start()
+
+    def column(line):
+        return jnp.broadcast_to(line, (LANES, tok_rows)).T[:, :1]
+
+    def normalize_rows(source, target, image, start, rows):
+        values = source[start : start + rows, :].astype(jnp.float32)
+        square = jnp.mean(values * values, axis=1, keepdims=True)
+        gains = jnp.where(
+            image[start : start + rows] > 0.5, gain_ref[1:2, :], gain_ref[0:1, :]
+        )
+        target[start : start + rows, :] = (
+            values * lax.rsqrt(square + epsilon) * gains
+        ).astype(jnp.bfloat16)
+
+    def pack(notes, rows, who, wave):
+        line = notes[pl.ds(who, 1), :]
+        slot = lax.broadcasted_iota(jnp.int32, (chunk, tok_rows), 0) + wave * chunk
+        pick = jnp.where(line == slot.astype(jnp.float32), 1.0, 0.0).astype(jnp.bfloat16)
+        return jnp.dot(pick, rows[...], preferred_element_type=jnp.float32).astype(jnp.bfloat16)
+
+    def feed(value):
+        opened = jnp.dot(value, gate[...], preferred_element_type=jnp.float32)
+        upper = jnp.dot(value, up[...], preferred_element_type=jnp.float32)
+        active = (opened / (1.0 + jnp.exp(-opened)) * upper).astype(jnp.bfloat16)
+        return jnp.dot(active, down[...], preferred_element_type=jnp.float32).astype(jnp.bfloat16)
+
+    def spots(notes, who):
+        line = column(notes[pl.ds(who, 1), :])
+        worth = column(notes[pl.ds(who + lines, 1), :])
+        slot = lax.broadcasted_iota(jnp.int32, (tok_rows, capacity), 1)
+        full = jnp.where(line == slot.astype(jnp.float32), worth, 0.0)
+        coarse = full.astype(jnp.bfloat16)
+        return coarse, (full - coarse.astype(jnp.float32)).astype(jnp.bfloat16)
+
+    def spread(coarse, fine, value):
+        return jnp.dot(coarse, value, preferred_element_type=jnp.float32) + jnp.dot(
+            fine, value, preferred_element_type=jnp.float32
+        )
+
+    image = column(facts[2 * lines : 2 * lines + 1, :])
+    rows = 64
+    for start in range(0, tok_rows, rows):
+        normalize_rows(tokens, normed, image, start, rows)
+
+    def send(wave):
+        packed[0, wave_rows(wave)] = pack(facts, normed, second, wave)
+        go(0, wave).start()
+
+    each(waves, send)
+
+    for load in loads[1:]:
+        load.wait()
+
+    def local(wave):
+        here = wave_rows(wave)
+        own_results[here] = feed(pack(facts, normed, me, wave))
+
+    each(waves, local)
+    total[...] = tokens[...].astype(jnp.float32) + spread(*spots(facts, me), own_results[...])
+
+    def serve(kind):
+        def step(wave):
+            here = wave_rows(wave)
+            go(kind, wave).wait_recv()
+            finished[kind, here] = feed(arrived[kind, here])
+            back(kind, wave).start()
+
+        each(waves, step)
+
+    serve(0)
+
+    told.wait_recv()
+    near_image = column(near_facts[2 * lines : 2 * lines + 1, :])
+    for block in range(blocks):
+        dense(block).wait_recv()
+        for start in range(block * part, (block + 1) * part, rows):
+            normalize_rows(near_tokens, near_normed, near_image, start, rows)
+
+    def forward(wave):
+        packed[1, wave_rows(wave)] = pack(near_facts, near_normed, second, wave)
+        go(1, wave).start()
+
+    each(waves, forward)
+
+    def near_local(wave):
+        here = wave_rows(wave)
+        own_rows[here] = feed(pack(near_facts, near_normed, me, wave))
+
+    each(waves, near_local)
+    near_total[...] = spread(*spots(near_facts, me), own_rows[...])
+
+    serve(1)
+
+    each(waves, lambda wave: back(0, wave).wait_recv())
+    total[...] += spread(*spots(facts, second), returned[0])
+
+    coarse, fine = spots(near_facts, second)
+    each(waves, lambda wave: back(1, wave).wait_recv())
+    for block in range(blocks):
+        here = slice(block * part, (block + 1) * part)
+        sum_out[here, :] = (
+            near_total[here, :] + spread(coarse[here], fine[here], returned[1])
+        ).astype(jnp.bfloat16)
+        sums(block).start()
+
+    for block in range(blocks):
+        here = slice(block * part, (block + 1) * part)
+        sums(block).wait_recv()
+        out_ref[here, :] = (total[here, :] + sum_in[here, :].astype(jnp.float32)).astype(
+            out_ref.dtype
+        )
+
+    told.wait_send()
+    each(blocks, lambda block: dense(block).wait_send())
+    each(blocks, lambda block: sums(block).wait_send())
+    for kind in range(2):
+        each(waves, lambda wave: go(kind, wave).wait_send())
+        each(waves, lambda wave: back(kind, wave).wait_send())
+
+
+def relay_scratch(tok_rows, width, hidden, capacity, waves, blocks):
+    dense = pltpu.VMEM((tok_rows, width), jnp.bfloat16)
+    sums = pltpu.VMEM((tok_rows, width), jnp.float32)
+    facts = pltpu.VMEM((24, tok_rows), jnp.float32)
+    slots = pltpu.VMEM((2, capacity, width), jnp.bfloat16)
+    single = pltpu.VMEM((capacity, width), jnp.bfloat16)
+    wide = pltpu.VMEM((width, hidden), jnp.bfloat16)
+    by_block = pltpu.SemaphoreType.DMA((blocks,))
+    by_wave = pltpu.SemaphoreType.DMA((2, waves))
+    return [
+        dense, dense, wide, wide, pltpu.VMEM((hidden, width), jnp.bfloat16), dense, dense,
+        sums, sums, facts, facts, slots, slots, slots, slots, single, single, dense, dense,
+        pltpu.SemaphoreType.DMA((4,)), pltpu.SemaphoreType.DMA((2,)), by_block, by_block,
+        by_wave, by_wave, by_wave, by_wave, by_block, by_block,
+    ]
+
+
+def direct_scratch(tok_rows, width, hidden, buffer, sems):
+    return [
+        pltpu.VMEM((tok_rows, width), jnp.bfloat16),
+        pltpu.VMEM((width, hidden), jnp.bfloat16),
+        pltpu.VMEM((width, hidden), jnp.bfloat16),
+        pltpu.VMEM((hidden, width), jnp.bfloat16),
+        pltpu.VMEM((tok_rows, width), jnp.bfloat16),
+        pltpu.VMEM((tok_rows, width), jnp.float32),
+        pltpu.VMEM((LANES, tok_rows), jnp.float32),
+        pltpu.VMEM((tok_rows, LANES), jnp.float32),
+        pltpu.VMEM((tok_rows, LANES), jnp.float32),
+        buffer,
+        buffer,
+        buffer,
+        buffer,
+        pltpu.SemaphoreType.DMA((4,)),
+        sems,
+        sems,
+        sems,
+        sems,
+    ]
+
+
 def shards(
     tokens, modality, expert_ids, route_weights, norm_gain, gate_weight, up_weight, down_weight
 ):
@@ -240,31 +552,20 @@
     near = pl.BlockSpec(memory_space=pltpu.VMEM)
     far = pl.BlockSpec(memory_space=pl.ANY)
     sems = pltpu.SemaphoreType.DMA((waves, devices))
+    blocks = 4
+    relayed = devices == 4 and tok_rows % (64 * blocks) == 0 and capacity % 32 == 0
+    if relayed:
+        kernel = functools.partial(relay_kernel, blocks)
+        scratch = relay_scratch(tok_rows, width, hidden, capacity, 2, blocks)
+    else:
+        kernel = functools.partial(moe_kernel, devices)
+        scratch = direct_scratch(tok_rows, width, hidden, buffer, sems)
     return pl.pallas_call(
-        functools.partial(moe_kernel, devices),
+        kernel,
         out_shape=jax.ShapeDtypeStruct((tok_rows, width), jnp.bfloat16),
         in_specs=[far, near, near, near, near, far, far, far],
         out_specs=near,
-        scratch_shapes=[
-            pltpu.VMEM((tok_rows, width), jnp.bfloat16),
-            pltpu.VMEM((width, hidden), jnp.bfloat16),
-            pltpu.VMEM((width, hidden), jnp.bfloat16),
-            pltpu.VMEM((hidden, width), jnp.bfloat16),
-            pltpu.VMEM((tok_rows, width), jnp.bfloat16),
-            pltpu.VMEM((tok_rows, width), jnp.float32),
-            pltpu.VMEM((LANES, tok_rows), jnp.float32),
-            pltpu.VMEM((tok_rows, LANES), jnp.float32),
-            pltpu.VMEM((tok_rows, LANES), jnp.float32),
-            buffer,
-            buffer,
-            buffer,
-            buffer,
-            pltpu.SemaphoreType.DMA((4,)),
-            sems,
-            sems,
-            sems,
-            sems,
-        ],
+        scratch_shapes=scratch,
         compiler_params=pltpu.CompilerParams(
             collective_id=0, has_side_effects=True, vmem_limit_bytes=62 * 1024 * 1024
         ),

time: 128 us -> 117 us (0.914)
  Pallas kernels: 125 us -> 113 us
    pallas_call x1, Pallas kernels: 125 us -> 113 us  [shards(): pl.pallas_call(kernel, out_shape=jax.ShapeDtypeStruct((tok_rows, width),...]
where the time goes in v2:
time: 117 us; the launch traced here: 116 us
  Pallas kernels  113 us (97%)
  local copies, waits for them, and re-layouts  3.16 us (3%)
    pallas_call x1, Pallas kernels, shards(): pl.pallas_call(kernel, out_shape=jax.ShapeDtypeStruct((tok_rows, width),...  113 us
    unnamed x1, local copies, waits for them, and re-layouts  3.16 us

profile of v2, /device:TPU:0, one launch (start us, length us, event | category | flops | bytes accessed | tf_op | source)
XLA Modules:
  0.0 116.5 jit_solution(7320536117164934296)
XLA Ops:
  0.0 113.3 %shard_map.82 = bf16[512,2048]{1,0:T(8,128)(2,1)} custom-call(bf16[512,2048]{1,0:T(8,128)(2,1)} %tokens_hbm.1, s32[1,512]{1,0:T(1,128)} %bitcast.5, s32[2,512]{1,0:T(2,128)} %bitcast.3, f32[2,512]{1,0:T(2,128)} %bitcast.4, f32[2,2048]{1,0:T(2,128)} %gain_ref.1, bf16[2048,896]{1,0:T(8,128)(2,1)} %gate_hbm.1, bf16[2048,896]{1,0:T(8,128)(2,1)} %up_hbm.1, ...), custom_call_target="tpu_custom_call" | custom-call | tf_op jit(solution)/shard_map/pallas_call | solution.py:563
  113.3 3.2 %copy.10 = bf16[512,2048]{1,0:T(8,128)(2,1)} copy(bf16[512,2048]{1,0:T(8,128)(2,1)} %shard_map.82) | data formatting | bytes 4194304

commit v3 on v2

--- a/solution.py
+++ b/solution.py
@@ -229,14 +229,18 @@
 def relay_kernel(
     blocks,
     tokens_hbm,
+    modality_hbm,
+    ids_hbm,
+    weights_hbm,
+    gain_hbm,
+    gate_hbm,
+    up_hbm,
+    down_hbm,
+    out_ref,
     modality_ref,
     ids_ref,
     weights_ref,
     gain_ref,
-    gate_hbm,
-    up_hbm,
-    down_hbm,
-    out_ref,
     tokens,
     near_tokens,
     gate,
@@ -257,6 +261,7 @@
     sum_out,
     sum_in,
     load_sem,
+    token_sem,
     facts_sem,
     dense_send,
     dense_recv,
@@ -337,22 +342,43 @@
         lax.fori_loop(0, count, body, 0)
 
     loads = [
-        pltpu.make_async_copy(tokens_hbm, tokens, load_sem.at[0]),
-        pltpu.make_async_copy(gate_hbm, gate, load_sem.at[1]),
-        pltpu.make_async_copy(up_hbm, up, load_sem.at[2]),
-        pltpu.make_async_copy(down_hbm, down, load_sem.at[3]),
+        pltpu.make_async_copy(source, target, load_sem.at[index])
+        for index, (source, target) in enumerate(
+            (
+                (ids_hbm, ids_ref),
+                (weights_hbm, weights_ref),
+                (modality_hbm, modality_ref),
+                (gain_hbm, gain_ref),
+                (gate_hbm, gate),
+                (up_hbm, up),
+                (down_hbm, down),
+            )
+        )
     ]
-    loads[0].start()
+
+    def token_load(block):
+        rows = part_rows(block)
+        return pltpu.make_async_copy(tokens_hbm.at[rows], tokens.at[rows], token_sem.at[block])
+
+    each(blocks, lambda block: token_load(block).start())
+    for load in loads[:4]:
+        load.start()
     barrier = pltpu.get_barrier_semaphore()
     for peer in (first, second):
         pl.semaphore_signal(
             barrier, inc=1, device_id={AXIS: peer}, device_id_type=pl.DeviceIdType.MESH
         )
-    loads[0].wait()
     pl.semaphore_wait(barrier, 2)
-    each(blocks, lambda block: dense(block).start())
-    for load in loads[1:]:
+
+    def leave(block):
+        token_load(block).wait()
+        dense(block).start()
+
+    each(blocks, leave)
+    for load in loads[4:]:
         load.start()
+    for load in loads[:4]:
+        load.wait()
 
     lines = 8
     expert = lax.broadcasted_iota(jnp.int32, (lines, tok_rows), 0)
@@ -428,7 +454,7 @@
 
     each(waves, send)
 
-    for load in loads[1:]:
+    for load in loads[4:]:
         load.wait()
 
     def local(wave):
@@ -438,16 +464,19 @@
     each(waves, local)
     total[...] = tokens[...].astype(jnp.float32) + spread(*spots(facts, me), own_results[...])
 
-    def serve(kind):
+    def serve(kind, now):
         def step(wave):
             here = wave_rows(wave)
             go(kind, wave).wait_recv()
             finished[kind, here] = feed(arrived[kind, here])
-            back(kind, wave).start()
+
+            @pl.when(wave < now)
+            def _():
+                back(kind, wave).start()
 
         each(waves, step)
 
-    serve(0)
+    serve(0, waves - 1)
 
     told.wait_recv()
     near_image = column(near_facts[2 * lines : 2 * lines + 1, :])
@@ -469,10 +498,8 @@
     each(waves, near_local)
     near_total[...] = spread(*spots(near_facts, me), own_rows[...])
 
-    serve(1)
-
-    each(waves, lambda wave: back(0, wave).wait_recv())
-    total[...] += spread(*spots(facts, second), returned[0])
+    serve(1, waves)
+    back(0, waves - 1).start()
 
     coarse, fine = spots(near_facts, second)
     each(waves, lambda wave: back(1, wave).wait_recv())
@@ -483,6 +510,9 @@
         ).astype(jnp.bfloat16)
         sums(block).start()
 
+    each(waves, lambda wave: back(0, wave).wait_recv())
+    total[...] += spread(*spots(facts, second), returned[0])
+
     for block in range(blocks):
         here = slice(block * part, (block + 1) * part)
         sums(block).wait_recv()
@@ -498,7 +528,7 @@
         each(waves, lambda wave: back(kind, wave).wait_send())
 
 
-def relay_scratch(tok_rows, width, hidden, capacity, waves, blocks):
+def relay_scratch(tok_rows, width, hidden, fanout, capacity, waves, blocks):
     dense = pltpu.VMEM((tok_rows, width), jnp.bfloat16)
     sums = pltpu.VMEM((tok_rows, width), jnp.float32)
     facts = pltpu.VMEM((24, tok_rows), jnp.float32)
@@ -508,9 +538,11 @@
     by_block = pltpu.SemaphoreType.DMA((blocks,))
     by_wave = pltpu.SemaphoreType.DMA((2, waves))
     return [
+        pltpu.VMEM((1, tok_rows), jnp.int32), pltpu.VMEM((fanout, tok_rows), jnp.int32),
+        pltpu.VMEM((fanout, tok_rows), jnp.float32), pltpu.VMEM((2, width), jnp.float32),
         dense, dense, wide, wide, pltpu.VMEM((hidden, width), jnp.bfloat16), dense, dense,
         sums, sums, facts, facts, slots, slots, slots, slots, single, single, dense, dense,
-        pltpu.SemaphoreType.DMA((4,)), pltpu.SemaphoreType.DMA((2,)), by_block, by_block,
+        pltpu.SemaphoreType.DMA((7,)), by_block, pltpu.SemaphoreType.DMA((2,)), by_block, by_block,
         by_wave, by_wave, by_wave, by_wave, by_block, by_block,
     ]
 
@@ -556,18 +588,18 @@
     relayed = devices == 4 and tok_rows % (64 * blocks) == 0 and capacity % 32 == 0
     if relayed:
         kernel = functools.partial(relay_kernel, blocks)
-        scratch = relay_scratch(tok_rows, width, hidden, capacity, 2, blocks)
+        scratch = relay_scratch(tok_rows, width, hidden, fanout, capacity, 2, blocks)
     else:
         kernel = functools.partial(moe_kernel, devices)
         scratch = direct_scratch(tok_rows, width, hidden, buffer, sems)
     return pl.pallas_call(
         kernel,
-        out_shape=jax.ShapeDtypeStruct((tok_rows, width), jnp.bfloat16),
-        in_specs=[far, near, near, near, near, far, far, far],
+        out_shape=pltpu.VMEM((tok_rows, width), jnp.bfloat16),
+        in_specs=[far] + [far if relayed else near] * 4 + [far] * 3,
         out_specs=near,
         scratch_shapes=scratch,
         compiler_params=pltpu.CompilerParams(
-            collective_id=0, has_side_effects=True, vmem_limit_bytes=62 * 1024 * 1024
+            collective_id=0, has_side_effects=True, vmem_limit_bytes=58 * 1024 * 1024
         ),
     )(
         tokens,

time: 117 us -> 114 us (0.974); the launches traced: 116 us -> 111 us
  Pallas kernels: 113 us -> 110 us
  local copies, waits for them, and re-layouts: 3.16 us -> 1.32 us
    pallas_call x1, Pallas kernels: 113 us -> 110 us  [shards(): pl.pallas_call(kernel, out_shape=pltpu.VMEM((tok_rows, width), jnp.bfloat...]
    unnamed x1, local copies, waits for them, and re-layouts: 3.16 us -> 1.32 us
where the time goes in v3:
time: 114 us; the launch traced here: 111 us
  Pallas kernels  110 us (96%)
  local copies, waits for them, and re-layouts  1.32 us (1%)
    pallas_call x1, Pallas kernels, shards(): pl.pallas_call(kernel, out_shape=pltpu.VMEM((tok_rows, width), jnp.bfloat...  110 us

profile of v3, /device:TPU:0, one launch (start us, length us, event | category | flops | bytes accessed | tf_op | source)
XLA Modules:
  0.0 111.4 jit_solution(9786516955363469599)
XLA Ops:
  0.0 110.1 %shard_map.82 = bf16[512,2048]{1,0:T(8,128)(2,1)S(1)} custom-call(bf16[512,2048]{1,0:T(8,128)(2,1)} %tokens_hbm.1, s32[1,512]{1,0:T(1,128)} %bitcast.5, s32[2,512]{1,0:T(2,128)} %bitcast.3, f32[2,512]{1,0:T(2,128)} %bitcast.4, f32[2,2048]{1,0:T(2,128)} %gain_hbm.1, bf16[2048,896]{1,0:T(8,128)(2,1)} %gate_hbm.1, bf16[2048,896]{1,0:T(8,128)(2,1)} %up_hbm.1, ...), custom_call_target="tpu_custom_call" | custom-call | tf_op jit(solution)/shard_map/pallas_call | solution.py:595
  110.1 1.3 %copy.10 = bf16[512,2048]{1,0:T(8,128)(2,1)} copy(bf16[512,2048]{1,0:T(8,128)(2,1)S(1)} %shard_map.82) | data formatting | bytes 4194304

commit v4 on v3

--- a/solution.py
+++ b/solution.py
@@ -300,6 +300,8 @@
         return pl.ds(pl.multiple_of(block * part, part), part)
 
     def wave_rows(wave):
+        if isinstance(wave, int):
+            return slice(wave * chunk, (wave + 1) * chunk)
         return pl.ds(pl.multiple_of(wave * chunk, chunk), chunk)
 
     def dense(block):
@@ -495,11 +497,14 @@
         here = wave_rows(wave)
         own_rows[here] = feed(pack(near_facts, near_normed, me, wave))
 
-    each(waves, near_local)
-    near_total[...] = spread(*spots(near_facts, me), own_rows[...])
+    near_local(0)
 
     serve(1, waves)
     back(0, waves - 1).start()
+
+    for wave in range(1, waves):
+        near_local(wave)
+    near_total[...] = spread(*spots(near_facts, me), own_rows[...])
 
     coarse, fine = spots(near_facts, second)
     each(waves, lambda wave: back(1, wave).wait_recv())

time: 114 us -> 114 us (level)
  no operation moved by 1% of the time
where the time goes in v4:
time: 114 us; the launch traced here: 111 us
  Pallas kernels  110 us (96%)
  local copies, waits for them, and re-layouts  1.32 us (1%)
    pallas_call x1, Pallas kernels, shards(): pl.pallas_call(kernel, out_shape=pltpu.VMEM((tok_rows, width), jnp.bfloat...  110 us

profile of v4, /device:TPU:0, one launch (start us, length us, event | category | flops | bytes accessed | tf_op | source)
XLA Modules:
  0.0 111.4 jit_solution(11431524748596542261)
XLA Ops:
  0.0 110.1 %shard_map.82 = bf16[512,2048]{1,0:T(8,128)(2,1)S(1)} custom-call(bf16[512,2048]{1,0:T(8,128)(2,1)} %tokens_hbm.1, s32[1,512]{1,0:T(1,128)} %bitcast.5, s32[2,512]{1,0:T(2,128)} %bitcast.3, f32[2,512]{1,0:T(2,128)} %bitcast.4, f32[2,2048]{1,0:T(2,128)} %gain_hbm.1, bf16[2048,896]{1,0:T(8,128)(2,1)} %gate_hbm.1, bf16[2048,896]{1,0:T(8,128)(2,1)} %up_hbm.1, ...), custom_call_target="tpu_custom_call" | custom-call | tf_op jit(solution)/shard_map/pallas_call | solution.py:600
  110.1 1.3 %copy.10 = bf16[512,2048]{1,0:T(8,128)(2,1)} copy(bf16[512,2048]{1,0:T(8,128)(2,1)S(1)} %shard_map.82) | data formatting | bytes 4194304
